TPU v7x, 32 devices: a whole 2x2x4 slice. The times are simulated.
32 devices in a mesh: member: 4 (over y, x), space: 8 (over z, core).
Axes of the slice: x: 2, y: 2, z: 4, core: 2. Of those that a mesh axis runs over, the one named last changes fastest.
Arguments:
- ensemble: float32 [128, 16, 16, 128], P(None, 'space', 'member'), may hold values from -4 to 4
- source: float32 [16, 16, 128], P('space', 'member'), may hold values from -6 to 6
- obs_rows: int32 [8, 4, 1], P('space', 'member'), may hold values from 0 to 7
- obs_values: float32 [8, 4, 128], P('space', 'member'), may hold values from -3 to 3
- obs_noise: float32 [128, 8, 4, 128], P(None, 'space', 'member'), may hold values from -5 to 5
- obs_var: float32 [8, 4, 128], P('space', 'member'), may hold values from 0.05 to 2
Outputs:
- updated: float32 [128, 16, 16, 128], P(None, 'space', 'member')
- predicted: float32 [128, 8, 4, 128], P(None, 'space', 'member')
Inputs may be any that keep to these rules, and one draw needn't show every extreme that they name: `obs_rows`: entry [s, m, o] names the cell row at (s * 2 + r // 4, m * 4 + r % 4) of the first two dimensions, whose 128 cells along the third dimension are observed; rows may repeat.
All inputs are finite; a program needn't handle non-finite values.
Results may differ from a plain program's by a relative error of at most 0.0003.
Values sent between devices are 32-bit elements; how exact they have to be, the bound alone decides.
No kernel may reach another device: no remote copies, remote signals or barrier semaphores. Data moves between devices by JAX's collectives and lax.ppermute only.
A program may use at most 64 MiB of HBM per device.

v0:
```python
import jax
import jax.numpy as jnp
from jax import lax
from jax.sharding import PartitionSpec as P

ITERS = 4


def padded_2(x, sides, width):
    for axis, dim in sides:
        devices, length = (lax.axis_size(axis), x.shape[dim])
        up = [(i, (i + 1) % devices) for i in range(devices - 1)]
        down = [(j, i) for i, j in up]
        last = lax.slice_in_dim(x, length - width, length, axis=dim)
        leading = lax.slice_in_dim(x, 0, width, axis=dim)
        before = lax.ppermute(last, axis, up)
        after = lax.ppermute(leading, axis, down)
        x = jnp.concatenate([before, x, after], axis=dim)
    return x


def harmonic(first_cond, second_cond):
    return 2.0 * first_cond * second_cond / (first_cond + second_cond)


def extend_cond(cond):
    widened = padded_2(cond, (("member", 2),), 1)
    return jnp.pad(widened, ((0, 0), (1, 1), (0, 0), (1, 1)))


def extend_values(values_in):
    widened = padded_2(values_in, (("member", 2),), 1)
    return jnp.pad(widened, ((0, 0), (1, 1), (0, 0), (1, 1)))


def member_dots(dot_terms):
    return lax.psum(dot_terms, "member")


def face_terms(cond):
    widened = extend_cond(cond)
    edge_pad = jnp.pad(cond, ((0, 0), (1, 1), (1, 1), (1, 1)), mode="edge")
    cond_pad = jnp.where(widened > 0.0, widened, edge_pad)
    face_x = harmonic(cond_pad[:, :-1, 1:-1, 1:-1], cond_pad[:, 1:, 1:-1, 1:-1])
    face_y = harmonic(cond_pad[:, 1:-1, :-1, 1:-1], cond_pad[:, 1:-1, 1:, 1:-1])
    face_z = harmonic(cond, cond_pad[:, 1:-1, 1:-1, 2:])
    lower_z = jnp.concatenate([harmonic(cond[..., :1], cond[..., :1]), face_z[..., :-1]], axis=-1)
    return (face_x, face_y, face_z, lower_z)


def operate(values_in, face_x, face_y, face_z, lower_z):
    padded = extend_values(values_in)
    result = face_x[:, 1:] * (values_in - padded[:, 2:, 1:-1, 1:-1]) + face_x[:, :-1] * (
        values_in - padded[:, :-2, 1:-1, 1:-1]
    )
    result = (
        result
        + face_y[:, :, 1:] * (values_in - padded[:, 1:-1, 2:, 1:-1])
        + face_y[:, :, :-1] * (values_in - padded[:, 1:-1, :-2, 1:-1])
    )
    result = (
        result
        + face_z * (values_in - padded[:, 1:-1, 1:-1, 2:])
        + lower_z * (values_in - padded[:, 1:-1, 1:-1, :-2])
    )
    return result


def conjugate(cond, forcing):
    face_x, face_y, face_z, lower_z = face_terms(cond)
    residual = jnp.broadcast_to(forcing[None], cond.shape)
    direction = residual
    solution = jnp.zeros_like(cond)
    norm_now = member_dots(jnp.sum(residual * residual, axis=(1, 2, 3)))
    for iteration in range(ITERS):
        image = operate(direction, face_x, face_y, face_z, lower_z)
        step_size = norm_now / member_dots(jnp.sum(direction * image, axis=(1, 2, 3)))
        solution = solution + step_size[:, None, None, None] * direction
        residual = residual - step_size[:, None, None, None] * image
        if iteration + 1 < ITERS:
            norm_next = member_dots(jnp.sum(residual * residual, axis=(1, 2, 3)))
            direction = residual + (norm_next / norm_now)[:, None, None, None] * direction
            norm_now = norm_next
    return solution


def local(ensemble, source, obs_rows, obs_values, obs_noise, obs_var):
    total_members = ensemble.shape[0]
    block_x, block_y, layers = source.shape
    held_fields = lax.all_to_all(ensemble, "space", split_axis=0, concat_axis=1, tiled=True)
    forcing = lax.all_gather(source, "space", axis=0, tiled=True)
    pressure = conjugate(jnp.exp(held_fields), forcing)
    held_count = pressure.shape[0]
    cells_flat = pressure.reshape(held_count, -1, layers)
    gathered_rows = lax.all_gather(obs_rows, "space", axis=0, tiled=True)
    row_ids = gathered_rows[:, 0]
    peer_ids = jnp.arange(row_ids.shape[0], dtype=jnp.int32)[:, None]
    flat_index = (peer_ids * block_x + row_ids // block_y) * block_y + row_ids % block_y
    picked = jnp.take(cells_flat, flat_index.reshape(-1), axis=1)
    returned = lax.all_to_all(picked, "space", split_axis=1, concat_axis=0, tiled=True)
    predicted = returned.reshape(total_members, 1, 1, -1)
    flat_pred = returned.reshape(total_members, -1)
    inv_sigma = 1.0 / jnp.sqrt(obs_var.reshape(-1))
    spread = (flat_pred - jnp.mean(flat_pred, axis=0)) * inv_sigma
    misfit = (obs_values.reshape(-1) - flat_pred) * inv_sigma + obs_noise.reshape(total_members, -1)
    gram_part = jnp.dot(spread, spread.T, precision=lax.Precision.HIGHEST)
    cross_part = jnp.dot(spread, misfit.T, precision=lax.Precision.HIGHEST)
    gram_sum, cross_sum = lax.psum((gram_part, cross_part), ("member", "space"))
    factor = jnp.linalg.cholesky(
        gram_sum + (total_members - 1.0) * jnp.eye(total_members, dtype=jnp.float32)
    )
    weights = jax.scipy.linalg.cho_solve((factor, True), cross_sum)
    flat_field = ensemble.reshape(total_members, -1)
    anomalies = flat_field - jnp.mean(flat_field, axis=0)
    updated = flat_field + jnp.dot(weights.T, anomalies, precision=lax.Precision.HIGHEST)
    return (updated.reshape(ensemble.shape), predicted)


def solution(mesh):
    in_specs = (
        P(None, "space", "member", None),
        P("space", "member", None),
        P("space", "member", None),
        P("space", "member", None),
        P(None, "space", "member", None),
        P("space", "member", None),
    )
    out_specs = (P(None, "space", "member", None), P(None, "space", "member", None))
    return jax.shard_map(local, mesh=mesh, in_specs=in_specs, out_specs=out_specs, check_vma=False)
```

profile of v0, /device:TPU:0, one launch (start us, length us, event | category | flops | bytes accessed | tf_op | source)
XLA Modules:
  0.0 352.0 jit_solution(3334532213000039188)
XLA Ops:
  7.2 6.4 %all-to-all-start = ((f32[128,2,4,128]{3,2,1,0:T(4,128)}), f32[128,2,4,128]{3,2,1,0:T(4,128)S(1)}, u32[]{:S(2)}, u32[]{:S(2)}) async-start(f32[128,2,4,128]{3,2,1,0:T(4,128)} %param.6), calls=%async_computation | async-start | bytes 1048576 | tf_op jit(solution)/shard_map/all_to_all | solution.py:90
  13.5 21.7 %all_gather.7 = f32[16,4,128]{2,1,0:T(4,128)S(1)} all-gather(f32[2,4,128]{2,1,0:T(4,128)} %param.7), channel_id=1, replica_groups=mesh['member'=4,'space'=8] {'space'}, dimensions={0}, use_global_device_ids=true | all-gather | bytes 36864 | tf_op jit(solution)/shard_map/all_gather | solution.py:91
  35.2 3.4 collective-permute-start.2
  41.9 4.8 %collective-permute-done.3 = f32[16,16,1,128]{3,0,2,1:T(8,128)S(1)} collective-permute-done((f32[16,16,1,128]{3,0,2,1:T(8,128)S(1)}, f32[16,16,1,128]{3,0,2,1:T(8,128)S(1)}, u32[]{:S(2)}, u32[]{:S(2)}) %collective-permute-start.3) | collective-permute-done | bytes 131104 | tf_op jit(solution)/shard_map/ppermute | solution.py:17
  47.3 1.7 select_maximum_fusion.6
  50.5 3.7 %collective-permute-start = (f32[16,16,1,128]{3,0,2,1:T(8,128)S(1)}, f32[16,16,1,128]{3,0,2,1:T(8,128)S(1)}, u32[]{:S(2)}, u32[]{:S(2)}) collective-permute-start(f32[16,16,1,128]{3,0,2,1:T(8,128)S(1)} %get-tuple-element.35), channel_id=1, source_target_pairs={{0,8},{8,16},{16,24},{1,9},{9,17},{17,25},{2,10},{10,18},{18,26},{... | collective-permute-start | bytes 393224 | tf_op jit(solution)/shard_map/ppermute | solution.py:16
  56.0 1.3 copy.25
  57.3 3.7 %collective-permute-done.1 = f32[16,16,1,128]{3,0,2,1:T(8,128)S(1)} collective-permute-done((f32[16,16,1,128]{3,0,2,1:T(8,128)S(1)}, f32[16,16,1,128]{3,0,2,1:T(8,128)S(1)}, u32[]{:S(2)}, u32[]{:S(2)}) %collective-permute-start.1) | collective-permute-done | bytes 131104 | tf_op jit(solution)/shard_map/ppermute | solution.py:17
  61.1 2.7 compare_select_fusion
  67.3 9.0 %all-reduce.7 = (f32[16]{0:T(128)S(1)}, f32[16]{0:T(128)S(1)}) all-reduce(f32[16]{0:T(128)S(1)} %reduce_sum.93, f32[16]{0:T(128)S(1)} %get-tuple-element.20), channel_id=1, replica_groups=mesh['member'=4,'space'=8] {'member'}, use_global_device_ids=true, to_apply=%region_1.2 | all-reduce | flops 32 | bytes 256 | tf_op jit(solution)/shard_map/psum | solution.py:37
  76.6 8.0 %psum.72 = f32[16]{0:T(128)S(1)} all-reduce(f32[16]{0:T(128)S(1)} %multiply_reduce_fusion.4), channel_id=1, replica_groups=mesh['member'=4,'space'=8] {'member'}, use_global_device_ids=true, to_apply=%region_5.6 | all-reduce | flops 16 | bytes 128 | tf_op jit(solution)/shard_map/psum | solution.py:37
  84.8 3.4 collective-permute-start.4
  90.7 4.5 %collective-permute-done.5 = f32[16,16,1,128]{3,0,2,1:T(8,128)S(1)} collective-permute-done((f32[16,16,1,128]{3,0,2,1:T(8,128)S(1)}, f32[16,16,1,128]{3,0,2,1:T(8,128)S(1)}, u32[]{:S(2)}, u32[]{:S(2)}) %collective-permute-start.5) | collective-permute-done | bytes 131104 | tf_op jit(solution)/shard_map/ppermute | solution.py:17
  95.6 1.4 multiply_reduce_fusion.3
  97.0 9.8 %psum.73 = f32[16]{0:T(128)S(1)} all-reduce(f32[16]{0:T(128)S(1)} %get-tuple-element.18), channel_id=1, replica_groups=mesh['member'=4,'space'=8] {'member'}, use_global_device_ids=true, to_apply=%region_7.8 | all-reduce | flops 16 | bytes 128 | tf_op jit(solution)/shard_map/psum | solution.py:37
  106.8 1.4 multiply_reduce_fusion.2
  108.2 8.0 %psum.74 = f32[16]{0:T(128)S(1)} all-reduce(f32[16]{0:T(128)S(1)} %get-tuple-element.16), channel_id=1, replica_groups=mesh['member'=4,'space'=8] {'member'}, use_global_device_ids=true, to_apply=%region_9.10 | all-reduce | flops 16 | bytes 128 | tf_op jit(solution)/shard_map/psum | solution.py:37
  117.0 3.5 collective-permute-start.6
  123.8 8.0 %all-reduce.5 = s32[8]{0:T(128)S(1)} all-reduce(s32[8]{0:T(128)S(1)} %bitcast_dynamic-update-slice_fusion), channel_id=1, replica_groups=mesh['member'=4,'space'=8] {'space'}, use_global_device_ids=true, to_apply=%add.5 | all-reduce | flops 8 | bytes 64 | tf_op jit(solution)/shard_map/squeeze | solution.py:96
  131.8 1.4 select_maximum_fusion.2
  133.2 2.3 multiply_reduce_fusion.1
  135.5 11.6 %psum.75 = f32[16]{0:T(128)S(1)} all-reduce(f32[16]{0:T(128)S(1)} %get-tuple-element.14), channel_id=1, replica_groups=mesh['member'=4,'space'=8] {'member'}, use_global_device_ids=true, to_apply=%region_11.12 | all-reduce | flops 16 | bytes 128 | tf_op jit(solution)/shard_map/psum | solution.py:37
  148.4 7.8 %psum.76 = f32[16]{0:T(128)S(1)} all-reduce(f32[16]{0:T(128)S(1)} %multiply_reduce_fusion), channel_id=1, replica_groups=mesh['member'=4,'space'=8] {'member'}, use_global_device_ids=true, to_apply=%region_13.14 | all-reduce | flops 16 | bytes 128 | tf_op jit(solution)/shard_map/psum | solution.py:37
  156.2 1.4 multiply_add_fusion.1
  157.6 3.7 %collective-permute-start.8 = (f32[16,16,1,128]{3,0,2,1:T(8,128)S(1)}, f32[16,16,1,128]{3,0,2,1:T(8,128)S(1)}, u32[]{:S(2)}, u32[]{:S(2)}) collective-permute-start(f32[16,16,1,128]{3,0,2,1:T(8,128)S(1)} %get-tuple-element.27), channel_id=1, source_target_pairs={{0,8},{8,16},{16,24},{1,9},{9,17},{17,25},{2,10},{10,18},{18,26},{... | collective-permute-start | bytes 393224 | tf_op jit(solution)/shard_map/ppermute | solution.py:16
  163.8 4.5 %collective-permute-done.9 = f32[16,16,1,128]{3,0,2,1:T(8,128)S(1)} collective-permute-done((f32[16,16,1,128]{3,0,2,1:T(8,128)S(1)}, f32[16,16,1,128]{3,0,2,1:T(8,128)S(1)}, u32[]{:S(2)}, u32[]{:S(2)}) %collective-permute-start.9) | collective-permute-done | bytes 131104 | tf_op jit(solution)/shard_map/ppermute | solution.py:17
  170.7 8.8 %psum.77 = f32[16]{0:T(128)S(1)} all-reduce(f32[16]{0:T(128)S(1)} %fusion.14), channel_id=1, replica_groups=mesh['member'=4,'space'=8] {'member'}, use_global_device_ids=true, to_apply=%region_15.16 | all-reduce | flops 16 | bytes 128 | tf_op jit(solution)/shard_map/psum | solution.py:37
  181.0 3.4 all-to-all-start.1
  184.7 5.6 %all-to-all-done.1 = f32[16,8,128]{2,0,1:T(8,128)S(1)} async-done(((f32[16,8,128]{2,0,1:T(8,128)}), f32[16,8,128]{2,0,1:T(8,128)S(1)}, u32[]{:S(2)}, u32[]{:S(2)}) %all-to-all-start.1) | async-done | bytes 65568 | tf_op jit(solution)/shard_map/all_to_all | solution.py:100
  192.5 124.4 %all-reduce.10.cloned.1.call-done = (f32[128,128]{1,0:T(8,128)}, f32[128,128]{1,0:T(8,128)}) async-done(((f32[128,128]{1,0:T(8,128)}, f32[128,128]{1,0:T(8,128)}), (f32[128,128]{1,0:T(8,128)}, f32[128,128]{1,0:T(8,128)})) %all-reduce.10.cloned.1.call-update) | async-done | bytes 131088 | tf_op jit(solution)/shard_map/psum | solution.py:108
  318.6 11.7 %cholesky.16 = f32[128,128]{1,0:T(8,128)S(1)} custom-call(f32[128,128]{1,0:T(8,128)S(1)} %fusion.73), custom_call_target="Cholesky" | custom-call | tf_op jit(solution)/shard_map/jit(cholesky)/cholesky | solution.py:109
  331.7 9.8 %custom-call.10 = f32[1,128,128]{1,2,0:T(8,128)S(1)} custom-call(f32[1,128,128]{2,1,0:T(8,128)S(1)} %fusion.67), custom_call_target="InvertDiagBlocksLowerTriangular" | custom-call | tf_op jit(solution)/shard_map/jit(_cho_solve)/triangular_solve | solution.py:112
  (106 shorter events, 34.4 us)
Async XLA Ops:
  7.2 41.8 %all-to-all-start = ((f32[128,2,4,128]{3,2,1,0:T(4,128)}), f32[128,2,4,128]{3,2,1,0:T(4,128)S(1)}, u32[]{:S(2)}, u32[]{:S(2)}) async-start(f32[128,2,4,128]{3,2,1,0:T(4,128)} %param.6), calls=%async_computation | async-start | bytes 1048576 | tf_op jit(solution)/shard_map/all_to_all | solution.py:90
  35.2 6.6 %collective-permute-start.2 = (f32[16,16,1,128]{3,0,2,1:T(8,128)S(1)}, f32[16,16,1,128]{3,0,2,1:T(8,128)S(1)}, u32[]{:S(2)}, u32[]{:S(2)}) collective-permute-start(f32[16,16,1,128]{3,0,2,1:T(8,128)S(1)} %broadcast_in_dim.16), channel_id=1, source_target_pairs={{0,8},{8,16},{16,24},{1,9},{9,17},{17,25},{2,10},{10,18},{18,26},{... | collective-permute-start | bytes 393224 | tf_op jit(solution)/shard_map/ppermute | solution.py:16
  38.7 8.0 %collective-permute-start.3 = (f32[16,16,1,128]{3,0,2,1:T(8,128)S(1)}, f32[16,16,1,128]{3,0,2,1:T(8,128)S(1)}, u32[]{:S(2)}, u32[]{:S(2)}) collective-permute-start(f32[16,16,1,128]{3,0,2,1:T(8,128)S(1)} %broadcast_in_dim.17), channel_id=1, source_target_pairs={{8,0},{16,8},{24,16},{9,1},{17,9},{25,17},{10,2},{18,10},{26,18},{... | collective-permute-start | bytes 393224 | tf_op jit(solution)/shard_map/ppermute | solution.py:17
  46.6 0.6 copy-start.7
  50.5 6.8 %collective-permute-start = (f32[16,16,1,128]{3,0,2,1:T(8,128)S(1)}, f32[16,16,1,128]{3,0,2,1:T(8,128)S(1)}, u32[]{:S(2)}, u32[]{:S(2)}) collective-permute-start(f32[16,16,1,128]{3,0,2,1:T(8,128)S(1)} %get-tuple-element.35), channel_id=1, source_target_pairs={{0,8},{8,16},{16,24},{1,9},{9,17},{17,25},{2,10},{10,18},{18,26},{... | collective-permute-start | bytes 393224 | tf_op jit(solution)/shard_map/ppermute | solution.py:16
  54.2 6.9 %collective-permute-start.1 = (f32[16,16,1,128]{3,0,2,1:T(8,128)S(1)}, f32[16,16,1,128]{3,0,2,1:T(8,128)S(1)}, u32[]{:S(2)}, u32[]{:S(2)}) collective-permute-start(f32[16,16,1,128]{3,0,2,1:T(8,128)S(1)} %get-tuple-element.36), channel_id=1, source_target_pairs={{8,0},{16,8},{24,16},{9,1},{17,9},{25,17},{10,2},{18,10},{26,18},{... | collective-permute-start | bytes 393224 | tf_op jit(solution)/shard_map/ppermute | solution.py:17
  64.2 1.5 copy-start
  64.2 1.6 copy-start.6
  64.2 1.6 copy-start.8
  66.7 28.9 %copy-start.2 = (f32[16,16,4,128]{3,0,2,1:T(8,128)}, f32[16,16,4,128]{3,0,2,1:T(8,128)S(1)}, u32[]{:S(2)}) copy-start(f32[16,16,4,128]{3,0,2,1:T(8,128)S(1)} %get-tuple-element.22) | copy-start | bytes 1572868
  84.8 5.9 %collective-permute-start.4 = (f32[16,16,1,128]{3,0,2,1:T(8,128)S(1)}, f32[16,16,1,128]{3,0,2,1:T(8,128)S(1)}, u32[]{:S(2)}, u32[]{:S(2)}) collective-permute-start(f32[16,16,1,128]{3,0,2,1:T(8,128)S(1)} %get-tuple-element.31), channel_id=1, source_target_pairs={{0,8},{8,16},{16,24},{1,9},{9,17},{17,25},{2,10},{10,18},{18,26},{... | collective-permute-start | bytes 393224 | tf_op jit(solution)/shard_map/ppermute | solution.py:16
  88.2 6.9 %collective-permute-start.5 = (f32[16,16,1,128]{3,0,2,1:T(8,128)S(1)}, f32[16,16,1,128]{3,0,2,1:T(8,128)S(1)}, u32[]{:S(2)}, u32[]{:S(2)}) collective-permute-start(f32[16,16,1,128]{3,0,2,1:T(8,128)S(1)} %get-tuple-element.32), channel_id=1, source_target_pairs={{8,0},{16,8},{24,16},{9,1},{17,9},{25,17},{10,2},{18,10},{26,18},{... | collective-permute-start | bytes 393224 | tf_op jit(solution)/shard_map/ppermute | solution.py:17
  106.8 15.7 %copy-start.12 = (u32[32]{0:T(128)S(1)}, u32[32]{0:T(128)}, u32[]{:S(2)}) copy-start(u32[32]{0:T(128)} %constant.131) | copy-start | bytes 388
  108.2 38.9 %copy-start.1 = (f32[16,16,4,128]{3,0,2,1:T(8,128)}, f32[16,16,4,128]{3,0,2,1:T(8,128)S(1)}, u32[]{:S(2)}) copy-start(f32[16,16,4,128]{3,0,2,1:T(8,128)S(1)} %get-tuple-element.17) | copy-start | bytes 1572868
  117.0 14.7 %collective-permute-start.6 = (f32[16,16,1,128]{3,0,2,1:T(8,128)}, f32[16,16,1,128]{3,0,2,1:T(8,128)S(1)}, u32[]{:S(2)}, u32[]{:S(2)}) collective-permute-start(f32[16,16,1,128]{3,0,2,1:T(8,128)} %get-tuple-element.29), channel_id=1, source_target_pairs={{0,8},{8,16},{16,24},{1,9},{9,17},{17,25},{2,10},{10,18},{18,26},{... | collective-permute-start | bytes 393224 | tf_op jit(solution)/shard_map/ppermute | solution.py:16
  120.6 11.2 %collective-permute-start.7 = (f32[16,16,1,128]{3,0,2,1:T(8,128)}, f32[16,16,1,128]{3,0,2,1:T(8,128)}, u32[]{:S(2)}, u32[]{:S(2)}) collective-permute-start(f32[16,16,1,128]{3,0,2,1:T(8,128)} %get-tuple-element.30), channel_id=1, source_target_pairs={{8,0},{16,8},{24,16},{9,1},{17,9},{25,17},{10,2},{18,10},{26,18},{... | collective-permute-start | bytes 393224 | tf_op jit(solution)/shard_map/ppermute | solution.py:17
  131.7 1.5 copy-start.3
  157.6 11.2 %copy-start.4 = (f32[16,16,4,128]{3,0,2,1:T(8,128)S(1)}, f32[16,16,4,128]{3,0,2,1:T(8,128)}, u32[]{:S(2)}) copy-start(f32[16,16,4,128]{3,0,2,1:T(8,128)} %copy-done.2) | copy-start | bytes 1572868
  157.6 6.2 %collective-permute-start.8 = (f32[16,16,1,128]{3,0,2,1:T(8,128)S(1)}, f32[16,16,1,128]{3,0,2,1:T(8,128)S(1)}, u32[]{:S(2)}, u32[]{:S(2)}) collective-permute-start(f32[16,16,1,128]{3,0,2,1:T(8,128)S(1)} %get-tuple-element.27), channel_id=1, source_target_pairs={{0,8},{8,16},{16,24},{1,9},{9,17},{17,25},{2,10},{10,18},{18,26},{... | collective-permute-start | bytes 393224 | tf_op jit(solution)/shard_map/ppermute | solution.py:16
  161.3 6.9 %collective-permute-start.9 = (f32[16,16,1,128]{3,0,2,1:T(8,128)S(1)}, f32[16,16,1,128]{3,0,2,1:T(8,128)S(1)}, u32[]{:S(2)}, u32[]{:S(2)}) collective-permute-start(f32[16,16,1,128]{3,0,2,1:T(8,128)S(1)} %get-tuple-element.28), channel_id=1, source_target_pairs={{8,0},{16,8},{24,16},{9,1},{17,9},{25,17},{10,2},{18,10},{26,18},{... | collective-permute-start | bytes 393224 | tf_op jit(solution)/shard_map/ppermute | solution.py:17
  169.4 15.2 %copy-start.11 = (f32[1,1,128]{2,1,0:T(1,128)S(1)}, f32[1,1,128]{2,1,0:T(1,128)}, u32[]{:S(2)}) copy-start(f32[1,1,128]{2,1,0:T(1,128)} %param.11) | copy-start | bytes 1540
  169.4 21.8 %copy-start.9 = (f32[128,1,1,128]{3,2,1,0:T(1,128)S(1)}, f32[128,1,1,128]{3,2,1,0:T(1,128)}, u32[]{:S(2)}) copy-start(f32[128,1,1,128]{3,2,1,0:T(1,128)} %param.10) | copy-start | bytes 196612
  169.4 21.8 %copy-start.10 = (f32[1,1,128]{2,1,0:T(1,128)S(1)}, f32[1,1,128]{2,1,0:T(1,128)}, u32[]{:S(2)}) copy-start(f32[1,1,128]{2,1,0:T(1,128)} %param.9) | copy-start | bytes 1540
  170.7 21.5 %copy-start.5 = (f32[128,2,4,128]{3,2,1,0:T(4,128)S(1)}, f32[128,2,4,128]{3,2,1,0:T(4,128)}, u32[]{:S(2)}) copy-start(f32[128,2,4,128]{3,2,1,0:T(4,128)} %param.6) | copy-start | bytes 1572868
  181.0 9.2 %all-to-all-start.1 = ((f32[16,8,128]{2,0,1:T(8,128)}), f32[16,8,128]{2,0,1:T(8,128)S(1)}, u32[]{:S(2)}, u32[]{:S(2)}) async-start(f32[16,8,128]{2,0,1:T(8,128)} %select_bitcast_fusion), calls=%async_computation.1 | async-start | bytes 131072 | tf_op jit(solution)/shard_map/all_to_all | solution.py:100
  184.4 132.4 %all-reduce.10.cloned.1.call-start = ((), (), s32[]{:S(2)}) async-start(), calls=%async_computation.2 | async-start | bytes 262144 | tf_op jit(solution)/shard_map/psum | solution.py:108
Sparse Core Ops, SparseCore 0:
  192.3 124.4 all-reduce.9
where the time goes:
time: 353 us; the launch traced here: 352 us
  waiting for transfers between devices  151 us (43%)
  blocking collectives  92.5 us (26%)
  other arithmetic  45.3 us (13%)
  starting transfers between devices  34.1 us (10%)
  between operations  15.2 us (4%)
  local copies, waits for them, and re-layouts  10.1 us (3%)
  matrix products  3.76 us (1%)
    psum x1, waiting for transfers between devices, local(): gram_sum, cross_sum = lax.psum((gram_part, cross_part), ('member', 'space'))  124 us
    psum x7, blocking collectives, member_dots(): return lax.psum(dot_terms, 'member')  62.8 us
    all_gather x1, blocking collectives, local(): forcing = lax.all_gather(source, 'space', axis=0, tiled=True)  21.7 us
    ppermute x5, starting transfers between devices, padded_2(): before = lax.ppermute(last, axis, up)  17.7 us
    ppermute x5, waiting for transfers between devices, padded_2(): after = lax.ppermute(leading, axis, down)  17.4 us
    another operation x3, other arithmetic, local(): jnp.linalg.cholesky(gram_sum + (total_members - 1.0) * jnp.eye(total_memb...  12.4 us
    another operation x2, other arithmetic, local(): weights = jax.scipy.linalg.cho_solve((factor, True), cross_sum)  10.5 us
    squeeze x1, blocking collectives, local(): row_ids = gathered_rows[:, 0]  7.97 us
  transfers between devices with their start and end apart: 13, of which 9 were waited for; matrix products, arithmetic and copies ran while one was open for 2% of the time, Pallas kernels for 0%

commit v1 on v0

--- a/solution.py
+++ b/solution.py
@@ -105,7 +105,7 @@
     misfit = (obs_values.reshape(-1) - flat_pred) * inv_sigma + obs_noise.reshape(total_members, -1)
     gram_part = jnp.dot(spread, spread.T, precision=lax.Precision.HIGHEST)
     cross_part = jnp.dot(spread, misfit.T, precision=lax.Precision.HIGHEST)
-    gram_sum, cross_sum = lax.psum((gram_part, cross_part), ("member", "space"))
+    gram_sum, cross_sum = lax.psum(lax.psum((gram_part, cross_part), "space"), "member")
     factor = jnp.linalg.cholesky(
         gram_sum + (total_members - 1.0) * jnp.eye(total_members, dtype=jnp.float32)
     )

time: 353 us -> 324 us (0.918)
  waiting for transfers between devices: 151 us -> 123 us
    psum x1 -> x2, waiting for transfers between devices: 124 us -> 96.3 us  [the longest x1 52.1 us: local(): lax.psum((gram_part, cross_part), 'space')]
  transfers between devices with their start and end apart: 13 -> 14, of which waited for: 9 -> 10; matrix products, arithmetic and copies ran while one was open for 2% -> 2% of each run, Pallas kernels for 0% -> 0%
where the time goes in v1:
time: 324 us; the launch traced here: 323 us
  waiting for transfers between devices  123 us (38%)
  blocking collectives  92.7 us (29%)
  other arithmetic  44.2 us (14%)
  starting transfers between devices  34.1 us (11%)
  between operations  15.2 us (5%)
  local copies, waits for them, and re-layouts  10.1 us (3%)
  matrix products  3.76 us (1%)
    psum x7, blocking collectives, member_dots(): return lax.psum(dot_terms, 'member')  63 us
    psum x1, waiting for transfers between devices, local(): lax.psum((gram_part, cross_part), 'space')  52.1 us
    psum x1, waiting for transfers between devices, local(): lax.psum(lax.psum((gram_part, cross_part), 'space'), 'member')  44.2 us
    all_gather x1, blocking collectives, local(): forcing = lax.all_gather(source, 'space', axis=0, tiled=True)  21.7 us
    ppermute x5, starting transfers between devices, padded_2(): before = lax.ppermute(last, axis, up)  17.7 us
    ppermute x5, waiting for transfers between devices, padded_2(): after = lax.ppermute(leading, axis, down)  17.3 us
    another operation x3, other arithmetic, local(): jnp.linalg.cholesky(gram_sum + (total_members - 1.0) * jnp.eye(total_memb...  12.4 us
    another operation x2, other arithmetic, local(): weights = jax.scipy.linalg.cho_solve((factor, True), cross_sum)  10.5 us
  transfers between devices with their start and end apart: 14, of which 10 were waited for; matrix products, arithmetic and copies ran while one was open for 2% of the time, Pallas kernels for 0%

profile of v1, /device:TPU:0, one launch (start us, length us, event | category | flops | bytes accessed | tf_op | source)
XLA Modules:
  0.0 323.2 jit_solution(3301064519038011832)
XLA Ops:
  7.2 6.4 %all-to-all-start = ((f32[128,2,4,128]{3,2,1,0:T(4,128)}), f32[128,2,4,128]{3,2,1,0:T(4,128)S(1)}, u32[]{:S(2)}, u32[]{:S(2)}) async-start(f32[128,2,4,128]{3,2,1,0:T(4,128)} %param.6), calls=%async_computation | async-start | bytes 1048576 | tf_op jit(solution)/shard_map/all_to_all | solution.py:90
  13.5 21.7 %all_gather.7 = f32[16,4,128]{2,1,0:T(4,128)S(1)} all-gather(f32[2,4,128]{2,1,0:T(4,128)} %param.7), channel_id=1, replica_groups=mesh['member'=4,'space'=8] {'space'}, dimensions={0}, use_global_device_ids=true | all-gather | bytes 36864 | tf_op jit(solution)/shard_map/all_gather | solution.py:91
  35.2 3.4 %collective-permute-start.2 = (f32[16,16,1,128]{3,0,2,1:T(8,128)S(1)}, f32[16,16,1,128]{3,0,2,1:T(8,128)S(1)}, u32[]{:S(2)}, u32[]{:S(2)}) collective-permute-start(f32[16,16,1,128]{3,0,2,1:T(8,128)S(1)} %broadcast_in_dim.16), channel_id=1, source_target_pairs={{0,8},{8,16},{16,24},{1,9},{9,17},{17,25},{2,10},{10,18},{18,26},{... | collective-permute-start | bytes 393224 | tf_op jit(solution)/shard_map/ppermute | solution.py:16
  41.9 4.8 %collective-permute-done.3 = f32[16,16,1,128]{3,0,2,1:T(8,128)S(1)} collective-permute-done((f32[16,16,1,128]{3,0,2,1:T(8,128)S(1)}, f32[16,16,1,128]{3,0,2,1:T(8,128)S(1)}, u32[]{:S(2)}, u32[]{:S(2)}) %collective-permute-start.3) | collective-permute-done | bytes 131104 | tf_op jit(solution)/shard_map/ppermute | solution.py:17
  47.3 1.7 select_maximum_fusion.6
  50.5 3.7 %collective-permute-start = (f32[16,16,1,128]{3,0,2,1:T(8,128)S(1)}, f32[16,16,1,128]{3,0,2,1:T(8,128)S(1)}, u32[]{:S(2)}, u32[]{:S(2)}) collective-permute-start(f32[16,16,1,128]{3,0,2,1:T(8,128)S(1)} %get-tuple-element.37), channel_id=1, source_target_pairs={{0,8},{8,16},{16,24},{1,9},{9,17},{17,25},{2,10},{10,18},{18,26},{... | collective-permute-start | bytes 393224 | tf_op jit(solution)/shard_map/ppermute | solution.py:16
  57.3 3.7 %collective-permute-done.1 = f32[16,16,1,128]{3,0,2,1:T(8,128)S(1)} collective-permute-done((f32[16,16,1,128]{3,0,2,1:T(8,128)S(1)}, f32[16,16,1,128]{3,0,2,1:T(8,128)S(1)}, u32[]{:S(2)}, u32[]{:S(2)}) %collective-permute-start.1) | collective-permute-done | bytes 131104 | tf_op jit(solution)/shard_map/ppermute | solution.py:17
  61.1 2.7 compare_select_fusion
  67.3 9.0 %all-reduce.7 = (f32[16]{0:T(128)S(1)}, f32[16]{0:T(128)S(1)}) all-reduce(f32[16]{0:T(128)S(1)} %reduce_sum.93, f32[16]{0:T(128)S(1)} %get-tuple-element.22), channel_id=1, replica_groups=mesh['member'=4,'space'=8] {'member'}, use_global_device_ids=true, to_apply=%region_1.2 | all-reduce | flops 32 | bytes 256 | tf_op jit(solution)/shard_map/psum | solution.py:37
  76.6 8.0 %psum.86 = f32[16]{0:T(128)S(1)} all-reduce(f32[16]{0:T(128)S(1)} %multiply_reduce_fusion.4), channel_id=1, replica_groups=mesh['member'=4,'space'=8] {'member'}, use_global_device_ids=true, to_apply=%region_5.6 | all-reduce | flops 16 | bytes 128 | tf_op jit(solution)/shard_map/psum | solution.py:37
  84.8 3.4 %collective-permute-start.4 = (f32[16,16,1,128]{3,0,2,1:T(8,128)S(1)}, f32[16,16,1,128]{3,0,2,1:T(8,128)S(1)}, u32[]{:S(2)}, u32[]{:S(2)}) collective-permute-start(f32[16,16,1,128]{3,0,2,1:T(8,128)S(1)} %get-tuple-element.33), channel_id=1, source_target_pairs={{0,8},{8,16},{16,24},{1,9},{9,17},{17,25},{2,10},{10,18},{18,26},{... | collective-permute-start | bytes 393224 | tf_op jit(solution)/shard_map/ppermute | solution.py:16
  90.7 4.5 %collective-permute-done.5 = f32[16,16,1,128]{3,0,2,1:T(8,128)S(1)} collective-permute-done((f32[16,16,1,128]{3,0,2,1:T(8,128)S(1)}, f32[16,16,1,128]{3,0,2,1:T(8,128)S(1)}, u32[]{:S(2)}, u32[]{:S(2)}) %collective-permute-start.5) | collective-permute-done | bytes 131104 | tf_op jit(solution)/shard_map/ppermute | solution.py:17
  95.6 1.4 multiply_reduce_fusion.3
  97.0 9.8 %psum.87 = f32[16]{0:T(128)S(1)} all-reduce(f32[16]{0:T(128)S(1)} %get-tuple-element.20), channel_id=1, replica_groups=mesh['member'=4,'space'=8] {'member'}, use_global_device_ids=true, to_apply=%region_7.8 | all-reduce | flops 16 | bytes 128 | tf_op jit(solution)/shard_map/psum | solution.py:37
  106.8 1.4 multiply_reduce_fusion.2
  108.2 8.0 %psum.88 = f32[16]{0:T(128)S(1)} all-reduce(f32[16]{0:T(128)S(1)} %get-tuple-element.18), channel_id=1, replica_groups=mesh['member'=4,'space'=8] {'member'}, use_global_device_ids=true, to_apply=%region_9.10 | all-reduce | flops 16 | bytes 128 | tf_op jit(solution)/shard_map/psum | solution.py:37
  117.0 3.5 %collective-permute-start.6 = (f32[16,16,1,128]{3,0,2,1:T(8,128)}, f32[16,16,1,128]{3,0,2,1:T(8,128)S(1)}, u32[]{:S(2)}, u32[]{:S(2)}) collective-permute-start(f32[16,16,1,128]{3,0,2,1:T(8,128)} %get-tuple-element.31), channel_id=1, source_target_pairs={{0,8},{8,16},{16,24},{1,9},{9,17},{17,25},{2,10},{10,18},{18,26},{... | collective-permute-start | bytes 393224 | tf_op jit(solution)/shard_map/ppermute | solution.py:16
  123.8 8.0 %all-reduce.5 = s32[8]{0:T(128)S(1)} all-reduce(s32[8]{0:T(128)S(1)} %bitcast_dynamic-update-slice_fusion), channel_id=1, replica_groups=mesh['member'=4,'space'=8] {'space'}, use_global_device_ids=true, to_apply=%add.5 | all-reduce | flops 8 | bytes 64 | tf_op jit(solution)/shard_map/squeeze | solution.py:96
  131.8 1.4 select_maximum_fusion.2
  133.2 2.3 multiply_reduce_fusion.1
  135.5 11.6 %psum.89 = f32[16]{0:T(128)S(1)} all-reduce(f32[16]{0:T(128)S(1)} %get-tuple-element.16), channel_id=1, replica_groups=mesh['member'=4,'space'=8] {'member'}, use_global_device_ids=true, to_apply=%region_11.12 | all-reduce | flops 16 | bytes 128 | tf_op jit(solution)/shard_map/psum | solution.py:37
  148.4 7.8 %psum.90 = f32[16]{0:T(128)S(1)} all-reduce(f32[16]{0:T(128)S(1)} %multiply_reduce_fusion), channel_id=1, replica_groups=mesh['member'=4,'space'=8] {'member'}, use_global_device_ids=true, to_apply=%region_13.14 | all-reduce | flops 16 | bytes 128 | tf_op jit(solution)/shard_map/psum | solution.py:37
  156.2 1.4 multiply_add_fusion.1
  157.6 3.7 %collective-permute-start.8 = (f32[16,16,1,128]{3,0,2,1:T(8,128)S(1)}, f32[16,16,1,128]{3,0,2,1:T(8,128)S(1)}, u32[]{:S(2)}, u32[]{:S(2)}) collective-permute-start(f32[16,16,1,128]{3,0,2,1:T(8,128)S(1)} %get-tuple-element.29), channel_id=1, source_target_pairs={{0,8},{8,16},{16,24},{1,9},{9,17},{17,25},{2,10},{10,18},{18,26},{... | collective-permute-start | bytes 393224 | tf_op jit(solution)/shard_map/ppermute | solution.py:16
  163.8 4.4 %collective-permute-done.9 = f32[16,16,1,128]{3,0,2,1:T(8,128)S(1)} collective-permute-done((f32[16,16,1,128]{3,0,2,1:T(8,128)S(1)}, f32[16,16,1,128]{3,0,2,1:T(8,128)S(1)}, u32[]{:S(2)}, u32[]{:S(2)}) %collective-permute-start.9) | collective-permute-done | bytes 131104 | tf_op jit(solution)/shard_map/ppermute | solution.py:17
  169.4 9.0 %psum.91 = f32[16]{0:T(128)S(1)} all-reduce(f32[16]{0:T(128)S(1)} %fusion.14), channel_id=1, replica_groups=mesh['member'=4,'space'=8] {'member'}, use_global_device_ids=true, to_apply=%region_15.16 | all-reduce | flops 16 | bytes 128 | tf_op jit(solution)/shard_map/psum | solution.py:37
  179.9 3.4 %all-to-all-start.1 = ((f32[16,8,128]{2,0,1:T(8,128)}), f32[16,8,128]{2,0,1:T(8,128)S(1)}, u32[]{:S(2)}, u32[]{:S(2)}) async-start(f32[16,8,128]{2,0,1:T(8,128)} %select_bitcast_fusion), calls=%async_computation.1 | async-start | bytes 131072 | tf_op jit(solution)/shard_map/all_to_all | solution.py:100
  183.4 5.8 %all-to-all-done.1 = f32[16,8,128]{2,0,1:T(8,128)S(1)} async-done(((f32[16,8,128]{2,0,1:T(8,128)}), f32[16,8,128]{2,0,1:T(8,128)S(1)}, u32[]{:S(2)}, u32[]{:S(2)}) %all-to-all-start.1) | async-done | bytes 65568 | tf_op jit(solution)/shard_map/all_to_all | solution.py:100
  191.7 52.1 %all-reduce.12.cloned.1.call-done = (f32[128,128]{1,0:T(8,128)}, f32[128,128]{1,0:T(8,128)}) async-done(((f32[128,128]{1,0:T(8,128)}, f32[128,128]{1,0:T(8,128)}), (f32[128,128]{1,0:T(8,128)}, f32[128,128]{1,0:T(8,128)})) %all-reduce.12.cloned.1.call-update) | async-done | bytes 131088 | tf_op jit(solution)/shard_map/psum | solution.py:108
  243.9 44.2 %all-reduce.14.cloned.1.call-done = (f32[128,128]{1,0:T(8,128)}, f32[128,128]{1,0:T(8,128)}) async-done(((f32[128,128]{1,0:T(8,128)}, f32[128,128]{1,0:T(8,128)}), (f32[128,128]{1,0:T(8,128)}, f32[128,128]{1,0:T(8,128)})) %all-reduce.14.cloned.1.call-update) | async-done | bytes 131088 | tf_op jit(solution)/shard_map/psum | solution.py:108
  289.9 11.7 %cholesky.16 = f32[128,128]{1,0:T(8,128)S(1)} custom-call(f32[128,128]{1,0:T(8,128)S(1)} %fusion.73), custom_call_target="Cholesky" | custom-call | tf_op jit(solution)/shard_map/jit(cholesky)/cholesky | solution.py:109
  302.9 9.8 %custom-call.10 = f32[1,128,128]{1,2,0:T(8,128)S(1)} custom-call(f32[1,128,128]{2,1,0:T(8,128)S(1)} %fusion.67), custom_call_target="InvertDiagBlocksLowerTriangular" | custom-call | tf_op jit(solution)/shard_map/jit(_cho_solve)/triangular_solve | solution.py:112
  (109 shorter events, 34.8 us)
Async XLA Ops:
  7.2 41.8 %all-to-all-start = ((f32[128,2,4,128]{3,2,1,0:T(4,128)}), f32[128,2,4,128]{3,2,1,0:T(4,128)S(1)}, u32[]{:S(2)}, u32[]{:S(2)}) async-start(f32[128,2,4,128]{3,2,1,0:T(4,128)} %param.6), calls=%async_computation | async-start | bytes 1048576 | tf_op jit(solution)/shard_map/all_to_all | solution.py:90
  35.2 6.6 %collective-permute-start.2 = (f32[16,16,1,128]{3,0,2,1:T(8,128)S(1)}, f32[16,16,1,128]{3,0,2,1:T(8,128)S(1)}, u32[]{:S(2)}, u32[]{:S(2)}) collective-permute-start(f32[16,16,1,128]{3,0,2,1:T(8,128)S(1)} %broadcast_in_dim.16), channel_id=1, source_target_pairs={{0,8},{8,16},{16,24},{1,9},{9,17},{17,25},{2,10},{10,18},{18,26},{... | collective-permute-start | bytes 393224 | tf_op jit(solution)/shard_map/ppermute | solution.py:16
  38.7 8.0 %collective-permute-start.3 = (f32[16,16,1,128]{3,0,2,1:T(8,128)S(1)}, f32[16,16,1,128]{3,0,2,1:T(8,128)S(1)}, u32[]{:S(2)}, u32[]{:S(2)}) collective-permute-start(f32[16,16,1,128]{3,0,2,1:T(8,128)S(1)} %broadcast_in_dim.17), channel_id=1, source_target_pairs={{8,0},{16,8},{24,16},{9,1},{17,9},{25,17},{10,2},{18,10},{26,18},{... | collective-permute-start | bytes 393224 | tf_op jit(solution)/shard_map/ppermute | solution.py:17
  46.6 0.6 copy-start.7
  50.5 6.8 %collective-permute-start = (f32[16,16,1,128]{3,0,2,1:T(8,128)S(1)}, f32[16,16,1,128]{3,0,2,1:T(8,128)S(1)}, u32[]{:S(2)}, u32[]{:S(2)}) collective-permute-start(f32[16,16,1,128]{3,0,2,1:T(8,128)S(1)} %get-tuple-element.37), channel_id=1, source_target_pairs={{0,8},{8,16},{16,24},{1,9},{9,17},{17,25},{2,10},{10,18},{18,26},{... | collective-permute-start | bytes 393224 | tf_op jit(solution)/shard_map/ppermute | solution.py:16
  54.2 6.9 %collective-permute-start.1 = (f32[16,16,1,128]{3,0,2,1:T(8,128)S(1)}, f32[16,16,1,128]{3,0,2,1:T(8,128)S(1)}, u32[]{:S(2)}, u32[]{:S(2)}) collective-permute-start(f32[16,16,1,128]{3,0,2,1:T(8,128)S(1)} %get-tuple-element.38), channel_id=1, source_target_pairs={{8,0},{16,8},{24,16},{9,1},{17,9},{25,17},{10,2},{18,10},{26,18},{... | collective-permute-start | bytes 393224 | tf_op jit(solution)/shard_map/ppermute | solution.py:17
  64.2 1.5 copy-start
  64.2 1.6 copy-start.6
  64.2 1.6 copy-start.8
  66.7 28.9 %copy-start.2 = (f32[16,16,4,128]{3,0,2,1:T(8,128)}, f32[16,16,4,128]{3,0,2,1:T(8,128)S(1)}, u32[]{:S(2)}) copy-start(f32[16,16,4,128]{3,0,2,1:T(8,128)S(1)} %get-tuple-element.24) | copy-start | bytes 1572868
  84.8 5.9 %collective-permute-start.4 = (f32[16,16,1,128]{3,0,2,1:T(8,128)S(1)}, f32[16,16,1,128]{3,0,2,1:T(8,128)S(1)}, u32[]{:S(2)}, u32[]{:S(2)}) collective-permute-start(f32[16,16,1,128]{3,0,2,1:T(8,128)S(1)} %get-tuple-element.33), channel_id=1, source_target_pairs={{0,8},{8,16},{16,24},{1,9},{9,17},{17,25},{2,10},{10,18},{18,26},{... | collective-permute-start | bytes 393224 | tf_op jit(solution)/shard_map/ppermute | solution.py:16
  88.2 6.9 %collective-permute-start.5 = (f32[16,16,1,128]{3,0,2,1:T(8,128)S(1)}, f32[16,16,1,128]{3,0,2,1:T(8,128)S(1)}, u32[]{:S(2)}, u32[]{:S(2)}) collective-permute-start(f32[16,16,1,128]{3,0,2,1:T(8,128)S(1)} %get-tuple-element.34), channel_id=1, source_target_pairs={{8,0},{16,8},{24,16},{9,1},{17,9},{25,17},{10,2},{18,10},{26,18},{... | collective-permute-start | bytes 393224 | tf_op jit(solution)/shard_map/ppermute | solution.py:17
  106.8 15.7 %copy-start.12 = (u32[32]{0:T(128)S(1)}, u32[32]{0:T(128)}, u32[]{:S(2)}) copy-start(u32[32]{0:T(128)} %constant.131) | copy-start | bytes 388
  108.2 38.9 %copy-start.1 = (f32[16,16,4,128]{3,0,2,1:T(8,128)}, f32[16,16,4,128]{3,0,2,1:T(8,128)S(1)}, u32[]{:S(2)}) copy-start(f32[16,16,4,128]{3,0,2,1:T(8,128)S(1)} %get-tuple-element.19) | copy-start | bytes 1572868
  117.0 14.7 %collective-permute-start.6 = (f32[16,16,1,128]{3,0,2,1:T(8,128)}, f32[16,16,1,128]{3,0,2,1:T(8,128)S(1)}, u32[]{:S(2)}, u32[]{:S(2)}) collective-permute-start(f32[16,16,1,128]{3,0,2,1:T(8,128)} %get-tuple-element.31), channel_id=1, source_target_pairs={{0,8},{8,16},{16,24},{1,9},{9,17},{17,25},{2,10},{10,18},{18,26},{... | collective-permute-start | bytes 393224 | tf_op jit(solution)/shard_map/ppermute | solution.py:16
  120.6 11.2 %collective-permute-start.7 = (f32[16,16,1,128]{3,0,2,1:T(8,128)}, f32[16,16,1,128]{3,0,2,1:T(8,128)}, u32[]{:S(2)}, u32[]{:S(2)}) collective-permute-start(f32[16,16,1,128]{3,0,2,1:T(8,128)} %get-tuple-element.32), channel_id=1, source_target_pairs={{8,0},{16,8},{24,16},{9,1},{17,9},{25,17},{10,2},{18,10},{26,18},{... | collective-permute-start | bytes 393224 | tf_op jit(solution)/shard_map/ppermute | solution.py:17
  131.7 1.5 copy-start.3
  157.6 11.1 %copy-start.4 = (f32[16,16,4,128]{3,0,2,1:T(8,128)S(1)}, f32[16,16,4,128]{3,0,2,1:T(8,128)}, u32[]{:S(2)}) copy-start(f32[16,16,4,128]{3,0,2,1:T(8,128)} %copy-done.2) | copy-start | bytes 1572868
  157.6 6.2 %collective-permute-start.8 = (f32[16,16,1,128]{3,0,2,1:T(8,128)S(1)}, f32[16,16,1,128]{3,0,2,1:T(8,128)S(1)}, u32[]{:S(2)}, u32[]{:S(2)}) collective-permute-start(f32[16,16,1,128]{3,0,2,1:T(8,128)S(1)} %get-tuple-element.29), channel_id=1, source_target_pairs={{0,8},{8,16},{16,24},{1,9},{9,17},{17,25},{2,10},{10,18},{18,26},{... | collective-permute-start | bytes 393224 | tf_op jit(solution)/shard_map/ppermute | solution.py:16
  161.3 6.9 %collective-permute-start.9 = (f32[16,16,1,128]{3,0,2,1:T(8,128)S(1)}, f32[16,16,1,128]{3,0,2,1:T(8,128)S(1)}, u32[]{:S(2)}, u32[]{:S(2)}) collective-permute-start(f32[16,16,1,128]{3,0,2,1:T(8,128)S(1)} %get-tuple-element.30), channel_id=1, source_target_pairs={{8,0},{16,8},{24,16},{9,1},{17,9},{25,17},{10,2},{18,10},{26,18},{... | collective-permute-start | bytes 393224 | tf_op jit(solution)/shard_map/ppermute | solution.py:17
  169.3 14.0 %copy-start.11 = (f32[1,1,128]{2,1,0:T(1,128)S(1)}, f32[1,1,128]{2,1,0:T(1,128)}, u32[]{:S(2)}) copy-start(f32[1,1,128]{2,1,0:T(1,128)} %param.11) | copy-start | bytes 1540
  169.3 20.7 %copy-start.9 = (f32[128,1,1,128]{3,2,1,0:T(1,128)S(1)}, f32[128,1,1,128]{3,2,1,0:T(1,128)}, u32[]{:S(2)}) copy-start(f32[128,1,1,128]{3,2,1,0:T(1,128)} %param.10) | copy-start | bytes 196612
  169.4 20.7 %copy-start.10 = (f32[1,1,128]{2,1,0:T(1,128)S(1)}, f32[1,1,128]{2,1,0:T(1,128)}, u32[]{:S(2)}) copy-start(f32[1,1,128]{2,1,0:T(1,128)} %param.9) | copy-start | bytes 1540
  169.4 22.0 %copy-start.5 = (f32[128,2,4,128]{3,2,1,0:T(4,128)S(1)}, f32[128,2,4,128]{3,2,1,0:T(4,128)}, u32[]{:S(2)}) copy-start(f32[128,2,4,128]{3,2,1,0:T(4,128)} %param.6) | copy-start | bytes 1572868
  179.9 9.2 %all-to-all-start.1 = ((f32[16,8,128]{2,0,1:T(8,128)}), f32[16,8,128]{2,0,1:T(8,128)S(1)}, u32[]{:S(2)}, u32[]{:S(2)}) async-start(f32[16,8,128]{2,0,1:T(8,128)} %select_bitcast_fusion), calls=%async_computation.1 | async-start | bytes 131072 | tf_op jit(solution)/shard_map/all_to_all | solution.py:100
  183.3 60.5 %all-reduce.12.cloned.1.call-start = ((), (), s32[]{:S(2)}) async-start(), calls=%async_computation.2 | async-start | bytes 262144 | tf_op jit(solution)/shard_map/psum | solution.py:108
  191.1 96.9 %all-reduce.14.cloned.1.call-start = ((), (), s32[]{:S(2)}) async-start(), calls=%async_computation.3 | async-start | bytes 262144 | tf_op jit(solution)/shard_map/psum | solution.py:108
Sparse Core Ops, SparseCore 0:
  191.2 52.5 all-reduce.11
  246.7 41.3 all-reduce.13
